TPU v7x, 512 devices: a whole 4x4x16 slice. The times are simulated.
512 devices in a mesh: gx: 8 (over y_hi, x), gy: 4 (over y_lo, core), gz: 16 (over z).
Axes of the slice: x: 4, y: 4 (y_hi: 2, y_lo: 2; y = y_hi * 2 + y_lo), z: 16, core: 2. Of those that a mesh axis runs over, the one named last changes fastest.
Arguments:
- fields: float32 [6, 128, 64, 2048], P(None, 'gx', 'gy', 'gz'), may hold values from -6 to 6
- permittivity: float32 [128, 64, 2048], P('gx', 'gy', 'gz'), may hold values from 1 to 4
- donor_owner: int32 [65536, 1], P(('gx', 'gy', 'gz')), may hold values from 0 to 63; in each aligned block of 128 rows (0 to 127, 128 to 255, ...) at most 4 rows name the same one
- donor_base: int32 [65536, 3], P(('gx', 'gy', 'gz')), may hold values from 0 to 127, as said below
- donor_weights: float32 [65536, 15], P(('gx', 'gy', 'gz')), may hold values from -3 to 3
Outputs:
- new_fields: float32 [6, 128, 64, 2048], P(None, 'gx', 'gy', 'gz')
- receptor_values: float32 [6, 65536], P(None, ('gx', 'gy', 'gz'))
Inputs may be any that keep to these rules, and one draw needn't show every extreme that they name: `donor_owner`: within the 128 rows of one device no owner index is named by more than 4 rows, and one is named by exactly 4. `donor_base`: column 0 lies in 0 to 15, column 1 in 0 to 15, column 2 in 0 to 127.
All inputs are finite; a program needn't handle non-finite values.
Results may differ from a plain program's by a relative error of at most 0.00002.
Values sent between devices are 32-bit elements; how exact they have to be, the bound alone decides.
No kernel may reach another device: no remote copies, remote signals or barrier semaphores. Data moves between devices by JAX's collectives and lax.ppermute only.
A program may use at most 192 MiB of HBM per device.

v0:
```python
import jax
import jax.numpy as jnp
from jax import lax
from jax.sharding import PartitionSpec as P

step_size = 0.25


def extended(array, sides, width):
    edges = {}
    for axis, dim in sides:
        size, length = (lax.axis_size(axis), array.shape[dim])
        up = [(i, (i + 1) % size) for i in range(size - 1)]
        last = lax.slice_in_dim(array, length - width, length, axis=dim)
        initial = lax.slice_in_dim(array, 0, width, axis=dim)
        edges[dim] = (
            lax.ppermute(last, axis, up),
            lax.ppermute(initial, axis, [(b, a) for a, b in up]),
        )
    done = []
    for _, dim in sides:
        low, high = edges[dim]
        around = [(width, width) if d in done else (0, 0) for d in range(array.ndim)]
        array = jnp.concatenate([jnp.pad(low, around), array, jnp.pad(high, around)], axis=dim)
        done.append(dim)
    return array


def padded_2(cells, sides, width):
    for axis, dim in sides:
        count = lax.axis_size(axis)
        ends = count - 1
        head = lax.slice_in_dim(cells, 0, width, axis=dim)
        tail = lax.slice_in_dim(cells, cells.shape[dim] - width, cells.shape[dim], axis=dim)
        cells = jnp.concatenate(
            [
                lax.ppermute(tail, axis, [(i, (i + 1) % count) for i in range(ends)]),
                cells,
                lax.ppermute(head, axis, [((i + 1) % count, i) for i in range(ends)]),
            ],
            axis=dim,
        )
    return cells


def shifted(field, axis_index, offset):
    window = [slice(2, -2), slice(2, -2), slice(2, -2)]
    length = field.shape[axis_index] - 4
    window[axis_index] = slice(2 + offset, 2 + offset + length)
    return field[tuple(window)]


def derivative(field, axis_index):
    outer = shifted(field, axis_index, -2) - shifted(field, axis_index, 2)
    inner = shifted(field, axis_index, 1) - shifted(field, axis_index, -1)
    return (outer + 8.0 * inner) / 12.0


def curl_rate(padded, coefficient):
    rate_ex = (derivative(padded[5], 1) - derivative(padded[4], 2)) / coefficient
    rate_ey = (derivative(padded[3], 2) - derivative(padded[5], 0)) / coefficient
    rate_ez = (derivative(padded[4], 0) - derivative(padded[3], 1)) / coefficient
    rate_hx = derivative(padded[1], 2) - derivative(padded[2], 1)
    rate_hy = derivative(padded[2], 0) - derivative(padded[0], 2)
    rate_hz = derivative(padded[0], 1) - derivative(padded[1], 0)
    return jnp.stack([rate_ex, rate_ey, rate_ez, rate_hx, rate_hy, rate_hz])


def contract(donor_tiles, weights):
    weight_x = weights[0:5]
    weight_y = weights[5:10]
    weight_z = weights[10:15]
    along_z = jnp.sum(donor_tiles * weight_z[None, None, None, :, :], axis=3)
    along_y = jnp.sum(along_z * weight_y[None, None, :, :], axis=2)
    return jnp.sum(along_y * weight_x[None, :, :], axis=1)


def gather_tiles(donor_grid, corner_rows):
    components, extent_x, extent_y, extent_z = donor_grid.shape
    flat_grid = donor_grid.reshape(components, extent_x * extent_y * extent_z)
    stencil = jnp.arange(5, dtype=jnp.int32)
    offsets = (
        stencil[:, None, None] * (extent_y * extent_z)
        + stencil[None, :, None] * extent_z
        + stencil[None, None, :]
    ).reshape(125)
    starts = corner_rows[0] * (extent_y * extent_z) + corner_rows[1] * extent_z + corner_rows[2]
    picked = jnp.take(flat_grid, offsets[:, None] + starts[None, :], axis=1)
    return picked.reshape(components, 5, 5, 5, corner_rows.shape[1])


def local(fields, permittivity, donor_owner, donor_base, donor_weights):
    accumulated = fields
    taylor_term = fields
    for power in range(1, 5):
        padded = extended(taylor_term, (("gx", 1), ("gy", 2), ("gz", 3)), 2)
        taylor_term = step_size / power * curl_rate(padded, permittivity)
        accumulated = accumulated + taylor_term
    donor_grid = padded_2(accumulated, (("gx", 1), ("gy", 2), ("gz", 3)), 2)
    group_size = lax.axis_size("gy") * lax.axis_size("gz")
    row_count = donor_owner.shape[0]
    capacity = 2 * row_count // group_size
    owner_id = donor_owner[:, 0]
    owner_hits = (owner_id[:, None] == jnp.arange(group_size, dtype=jnp.int32)[None, :]).astype(
        jnp.int32
    )
    earlier = jnp.cumsum(owner_hits, axis=0) - owner_hits
    slot_index = jnp.sum(earlier * owner_hits, axis=1)
    flat_index = owner_id * capacity + slot_index
    corner_send = (
        jnp.zeros((3, group_size * capacity), jnp.int32).at[:, flat_index].set(donor_base.T)
    )
    corner_send = corner_send.reshape(3, group_size, capacity)
    weight_send = (
        jnp.zeros((15, group_size * capacity), jnp.float32).at[:, flat_index].set(donor_weights.T)
    )
    weight_send = weight_send.reshape(15, group_size, capacity)
    donor_corners = lax.all_to_all(
        corner_send, ("gy", "gz"), split_axis=1, concat_axis=1, tiled=True
    )
    piece_weights = lax.all_to_all(
        weight_send, ("gy", "gz"), split_axis=1, concat_axis=1, tiled=True
    )
    slot_count = donor_corners.shape[2]
    donor_tiles = gather_tiles(donor_grid, donor_corners.reshape(3, -1))
    values = contract(donor_tiles, piece_weights.reshape(15, -1)).reshape(6, group_size, slot_count)
    answers = lax.all_to_all(values, ("gy", "gz"), split_axis=1, concat_axis=1, tiled=True)
    receptor_values = answers.reshape(6, -1)[:, flat_index]
    return (accumulated, receptor_values)


def solution(mesh):
    placed = (
        P(None, "gx", "gy", "gz"),
        P("gx", "gy", "gz"),
        P(("gx", "gy", "gz"), None),
        P(("gx", "gy", "gz"), None),
        P(("gx", "gy", "gz"), None),
    )
    return jax.shard_map(
        local,
        mesh=mesh,
        in_specs=placed,
        out_specs=(P(None, "gx", "gy", "gz"), P(None, ("gx", "gy", "gz"))),
        check_vma=False,
    )
```

profile of v0, /device:TPU:14, one launch (start us, length us, event | category | flops | bytes accessed | tf_op | source)
XLA Modules:
  0.0 377.5 jit_solution(17785123580572100083)
XLA Ops:
  3.0 3.8 %collective-permute-start = (f32[6,16,16,2]{2,1,3,0:T(8,128)S(1)}, f32[6,16,16,2]{2,1,3,0:T(8,128)S(1)}, u32[]{:S(2)}, u32[]{:S(2)}) collective-permute-start(f32[6,16,16,2]{2,1,3,0:T(8,128)S(1)} %copy.153), channel_id=1, source_target_pairs={{0,1},{1,2},{2,3},{3,4},{4,5},{5,6},{6,7},{7,8},{8,9},{9,10},{10,1... | collective-permute-start | bytes 36872 | tf_op jit(solution)/shard_map/ppermute | solution.py:17
  10.8 3.6 collective-permute-start.4
  14.5 4.1 %collective-permute-start.2 = (f32[6,2,16,128]{3,2,1,0:T(8,128)S(1)}, f32[6,2,16,128]{3,2,1,0:T(8,128)S(1)}, u32[]{:S(2)}, u32[]{:S(2)}) collective-permute-start(f32[6,2,16,128]{3,2,1,0:T(8,128)S(1)} %get-tuple-element.60), channel_id=1, source_target_pairs={{0,64},{64,128},{128,192},{192,256},{256,320},{320,384},{384,448},... | collective-permute-start | bytes 294920 | tf_op jit(solution)/shard_map/ppermute | solution.py:17
  21.3 19.1 %all-to-all-start = ((s32[3,64,4]{2,0,1:T(4,128)}), s32[3,64,4]{2,0,1:T(4,128)S(1)}, u32[]{:S(2)}, u32[]{:S(2)}) async-start(s32[3,64,4]{2,0,1:T(4,128)} %copy.142), calls=%async_computation | async-start | bytes 262144 | tf_op jit(solution)/shard_map/all_to_all | solution.py:118
  43.8 7.3 %collective-permute-done.3 = f32[6,2,16,128]{3,2,1,0:T(8,128)S(1)} collective-permute-done((f32[6,2,16,128]{3,2,1,0:T(8,128)S(1)}, f32[6,2,16,128]{3,2,1,0:T(8,128)S(1)}, u32[]{:S(2)}, u32[]{:S(2)}) %collective-permute-start.3) | collective-permute-done | bytes 98336 | tf_op jit(solution)/shard_map/ppermute | solution.py:18
  60.5 3.9 %collective-permute-start.6 = (f32[6,16,16,2]{2,1,3,0:T(8,128)}, f32[6,16,16,2]{2,1,3,0:T(8,128)}, u32[]{:S(2)}, u32[]{:S(2)}) collective-permute-start(f32[6,16,16,2]{2,1,3,0:T(8,128)} %copy.117), channel_id=1, source_target_pairs={{0,1},{1,2},{2,3},{3,4},{4,5},{5,6},{6,7},{7,8},{8,9},{9,10},{10,1... | collective-permute-start | bytes 36872 | tf_op jit(solution)/shard_map/ppermute | solution.py:17
  71.7 3.6 collective-permute-start.10
  77.3 3.9 %collective-permute-start.9 = (f32[6,2,16,128]{3,2,1,0:T(8,128)}, f32[6,2,16,128]{3,2,1,0:T(8,128)}, u32[]{:S(2)}, u32[]{:S(2)}) collective-permute-start(f32[6,2,16,128]{3,2,1,0:T(8,128)} %get-tuple-element.55), channel_id=1, source_target_pairs={{64,0},{128,64},{192,128},{256,192},{320,256},{384,320},{448,384},... | collective-permute-start | bytes 294920 | tf_op jit(solution)/shard_map/ppermute | solution.py:18
  99.2 5.2 %collective-permute-start.12 = (f32[6,16,16,2]{2,1,3,0:T(8,128)}, f32[6,16,16,2]{2,1,3,0:T(8,128)}, u32[]{:S(2)}, u32[]{:S(2)}) collective-permute-start(f32[6,16,16,2]{2,1,3,0:T(8,128)} %copy.125), channel_id=1, source_target_pairs={{0,1},{1,2},{2,3},{3,4},{4,5},{5,6},{6,7},{7,8},{8,9},{9,10},{10,1... | collective-permute-start | bytes 36872 | tf_op jit(solution)/shard_map/ppermute | solution.py:17
  116.5 5.5 %collective-permute-start.14 = (f32[6,2,16,128]{3,2,1,0:T(8,128)}, f32[6,2,16,128]{3,2,1,0:T(8,128)}, u32[]{:S(2)}, u32[]{:S(2)}) collective-permute-start(f32[6,2,16,128]{3,2,1,0:T(8,128)} %get-tuple-element.48), channel_id=1, source_target_pairs={{0,64},{64,128},{128,192},{192,256},{256,320},{320,384},{384,448},... | collective-permute-start | bytes 294920 | tf_op jit(solution)/shard_map/ppermute | solution.py:17
  122.0 15.8 %all-to-all-start.1 = ((f32[15,64,4]{0,2,1:T(4,128)}), f32[15,64,4]{0,2,1:T(4,128)S(1)}, u32[]{:S(2)}, u32[]{:S(2)}) async-start(f32[15,64,4]{0,2,1:T(4,128)} %bitcast.55), calls=%async_computation.1 | async-start | bytes 262144 | tf_op jit(solution)/shard_map/all_to_all | solution.py:121
  159.6 4.0 %collective-permute-start.18 = (f32[6,16,16,2]{2,1,3,0:T(8,128)}, f32[6,16,16,2]{2,1,3,0:T(8,128)}, u32[]{:S(2)}, u32[]{:S(2)}) collective-permute-start(f32[6,16,16,2]{2,1,3,0:T(8,128)} %copy.133), channel_id=1, source_target_pairs={{0,1},{1,2},{2,3},{3,4},{4,5},{5,6},{6,7},{7,8},{8,9},{9,10},{10,1... | collective-permute-start | bytes 36872 | tf_op jit(solution)/shard_map/ppermute | solution.py:17
  172.1 3.6 collective-permute-start.22
  175.7 7.1 %collective-permute-start.20 = (f32[6,2,16,128]{3,2,1,0:T(8,128)}, f32[6,2,16,128]{3,2,1,0:T(8,128)}, u32[]{:S(2)}, u32[]{:S(2)}) collective-permute-start(f32[6,2,16,128]{3,2,1,0:T(8,128)} %get-tuple-element.42), channel_id=1, source_target_pairs={{0,64},{64,128},{128,192},{192,256},{256,320},{320,384},{384,448},... | collective-permute-start | bytes 294920 | tf_op jit(solution)/shard_map/ppermute | solution.py:17
  199.2 7.5 %collective-permute-start.24 = (f32[6,2,16,128]{3,2,1,0:T(8,128)S(1)}, f32[6,2,16,128]{3,2,1,0:T(8,128)S(1)}, u32[]{:S(2)}, u32[]{:S(2)}) collective-permute-start(f32[6,2,16,128]{3,2,1,0:T(8,128)S(1)} %get-tuple-element.40), channel_id=1, source_target_pairs={{0,64},{64,128},{128,192},{192,256},{256,320},{320,384},{384,448},... | collective-permute-start | bytes 294920 | tf_op jit(solution)/shard_map/ppermute | solution.py:37
  208.9 7.9 %collective-permute-done.25 = f32[6,2,16,128]{3,2,1,0:T(8,128)S(1)} collective-permute-done((f32[6,2,16,128]{3,2,1,0:T(8,128)S(1)}, f32[6,2,16,128]{3,2,1,0:T(8,128)S(1)}, u32[]{:S(2)}, u32[]{:S(2)}) %collective-permute-start.25) | collective-permute-done | bytes 98336 | tf_op jit(solution)/shard_map/ppermute | solution.py:39
  218.9 3.6 collective-permute-start.27
  229.8 5.2 %collective-permute-start.28 = (f32[6,20,20,2]{2,1,3,0:T(8,128)}, f32[6,20,20,2]{2,1,3,0:T(8,128)}, u32[]{:S(2)}, u32[]{:S(2)}) collective-permute-start(f32[6,20,20,2]{2,1,3,0:T(8,128)} %copy.157), channel_id=1, source_target_pairs={{0,1},{1,2},{2,3},{3,4},{4,5},{5,6},{6,7},{7,8},{8,9},{9,10},{10,1... | collective-permute-start | bytes 57608 | tf_op jit(solution)/shard_map/ppermute | solution.py:37
  246.8 4.7 %pad_maximum_fusion = f32[6,20,20,132]{3,2,1,0:T(8,128)} fusion(f32[6,20,20,2]{3,2,1,0:T(8,128)} %copy.146, f32[6,20,2,128]{3,2,1,0:T(2,128)S(1)} %collective-permute-done.27, f32[6,2,16,128]{3,2,1,0:T(8,128)S(1)} %collective-permute-done.25, f32[6,16,16,128]{3,2,1,0:T(8,128)S(1)} %multiply_add_fusion, f32[6,2,16,128]{3,2,1,0:T(8,128)S(1)} %collective-permute-done.24, ...), kind=kLoop, calls=%fused_computation.32 | loop fusion | flops 1900800 | bytes 2534400 | tf_op jit(solution)/shard_map/concatenate | solution.py:35
  254.9 14.0 %copy.147 = f32[6,52800]{0,1:T(8,128)} copy(f32[6,52800]{1,0:T(8,128)S(1)} %reshape.199) | data formatting | bytes 2534400 | tf_op jit(solution)/shard_map/reshape | solution.py:80
  268.8 67.8 %gather_fusion = f32[32000,6]{1,0:T(8,128)} fusion(f32[6,52800]{0,1:T(8,128)} %copy.147, s32[32768]{0:T(1024)S(1)} %pad_clamp_fusion), kind=kCustom, calls=%fused_computation | custom fusion | bytes 1664000 | tf_op jit(solution)/shard_map/jit(_take)/gather | solution.py:88
  336.7 7.9 %multiply_reduce_fusion = f32[6,5,5,256]{0,3,2,1:T(8,128)S(1)} fusion(f32[6,5,5,5,256]{0,4,3,2,1:T(8,128)} %bitcast.166, f32[5,256]{1,0:T(8,128)S(1)} %copy.149, pred[5,5,5,256]{3,2,1,0:T(8,128)(4,1)S(1)} %fusion.10), kind=kLoop, calls=%fused_computation.4 | loop fusion | flops 537600 | bytes 958720 | tf_op jit(solution)/shard_map/reduce_sum | solution.py:73
  345.9 13.9 %all-to-all-start.2 = ((f32[6,64,4]{0,2,1:T(4,128)}), f32[6,64,4]{0,2,1:T(4,128)S(1)}, u32[]{:S(2)}, u32[]{:S(2)}) async-start(f32[6,64,4]{0,2,1:T(4,128)} %bitcast.59), calls=%async_computation.2 | async-start | bytes 262144 | tf_op jit(solution)/shard_map/all_to_all | solution.py:127
  359.8 16.4 %all-to-all-done.2 = f32[6,64,4]{0,2,1:T(4,128)S(1)} async-done(((f32[6,64,4]{0,2,1:T(4,128)}), f32[6,64,4]{0,2,1:T(4,128)S(1)}, u32[]{:S(2)}, u32[]{:S(2)}) %all-to-all-start.2) | async-done | bytes 6176 | tf_op jit(solution)/shard_map/all_to_all | solution.py:127
  (183 shorter events, 136.2 us)
Async XLA Ops:
  3.0 37.4 %collective-permute-start = (f32[6,16,16,2]{2,1,3,0:T(8,128)S(1)}, f32[6,16,16,2]{2,1,3,0:T(8,128)S(1)}, u32[]{:S(2)}, u32[]{:S(2)}) collective-permute-start(f32[6,16,16,2]{2,1,3,0:T(8,128)S(1)} %copy.153), channel_id=1, source_target_pairs={{0,1},{1,2},{2,3},{3,4},{4,5},{5,6},{6,7},{7,8},{8,9},{9,10},{10,1... | collective-permute-start | bytes 36872 | tf_op jit(solution)/shard_map/ppermute | solution.py:17
  7.5 35.6 %collective-permute-start.5 = (f32[6,16,16,2]{2,1,3,0:T(8,128)S(1)}, f32[6,16,16,2]{2,1,3,0:T(8,128)S(1)}, u32[]{:S(2)}, u32[]{:S(2)}) collective-permute-start(f32[6,16,16,2]{2,1,3,0:T(8,128)S(1)} %copy.156), channel_id=1, source_target_pairs={{1,0},{2,1},{3,2},{4,3},{5,4},{6,5},{7,6},{8,7},{9,8},{10,9},{11,1... | collective-permute-start | bytes 36872 | tf_op jit(solution)/shard_map/ppermute | solution.py:18
  8.9 34.8 %collective-permute-start.1 = (f32[6,16,2,128]{3,1,2,0:T(8,128)S(1)}, f32[6,16,2,128]{3,1,2,0:T(8,128)S(1)}, u32[]{:S(2)}, u32[]{:S(2)}) collective-permute-start(f32[6,16,2,128]{3,1,2,0:T(8,128)S(1)} %copy.154), channel_id=1, source_target_pairs={{0,16},{16,32},{32,48},{1,17},{17,33},{33,49},{2,18},{18,34},{34,5... | collective-permute-start | bytes 294920 | tf_op jit(solution)/shard_map/ppermute | solution.py:17
  10.8 32.9 %collective-permute-start.4 = (f32[6,16,2,128]{3,1,2,0:T(8,128)S(1)}, f32[6,16,2,128]{3,1,2,0:T(8,128)S(1)}, u32[]{:S(2)}, u32[]{:S(2)}) collective-permute-start(f32[6,16,2,128]{3,1,2,0:T(8,128)S(1)} %copy.155), channel_id=1, source_target_pairs={{16,0},{32,16},{48,32},{17,1},{33,17},{49,33},{18,2},{34,18},{50,3... | collective-permute-start | bytes 294920 | tf_op jit(solution)/shard_map/ppermute | solution.py:18
  14.5 29.3 %collective-permute-start.2 = (f32[6,2,16,128]{3,2,1,0:T(8,128)S(1)}, f32[6,2,16,128]{3,2,1,0:T(8,128)S(1)}, u32[]{:S(2)}, u32[]{:S(2)}) collective-permute-start(f32[6,2,16,128]{3,2,1,0:T(8,128)S(1)} %get-tuple-element.60), channel_id=1, source_target_pairs={{0,64},{64,128},{128,192},{192,256},{256,320},{320,384},{384,448},... | collective-permute-start | bytes 294920 | tf_op jit(solution)/shard_map/ppermute | solution.py:17
  21.3 100.8 %all-to-all-start = ((s32[3,64,4]{2,0,1:T(4,128)}), s32[3,64,4]{2,0,1:T(4,128)S(1)}, u32[]{:S(2)}, u32[]{:S(2)}) async-start(s32[3,64,4]{2,0,1:T(4,128)} %copy.142), calls=%async_computation | async-start | bytes 262144 | tf_op jit(solution)/shard_map/all_to_all | solution.py:118
  60.5 16.8 %collective-permute-start.6 = (f32[6,16,16,2]{2,1,3,0:T(8,128)}, f32[6,16,16,2]{2,1,3,0:T(8,128)}, u32[]{:S(2)}, u32[]{:S(2)}) collective-permute-start(f32[6,16,16,2]{2,1,3,0:T(8,128)} %copy.117), channel_id=1, source_target_pairs={{0,1},{1,2},{2,3},{3,4},{4,5},{5,6},{6,7},{7,8},{8,9},{9,10},{10,1... | collective-permute-start | bytes 36872 | tf_op jit(solution)/shard_map/ppermute | solution.py:17
  66.3 18.6 %collective-permute-start.11 = (f32[6,16,16,2]{2,1,3,0:T(8,128)}, f32[6,16,16,2]{2,1,3,0:T(8,128)}, u32[]{:S(2)}, u32[]{:S(2)}) collective-permute-start(f32[6,16,16,2]{2,1,3,0:T(8,128)} %copy.122), channel_id=1, source_target_pairs={{1,0},{2,1},{3,2},{4,3},{5,4},{6,5},{7,6},{8,7},{9,8},{10,9},{11,1... | collective-permute-start | bytes 36872 | tf_op jit(solution)/shard_map/ppermute | solution.py:18
  69.1 18.2 %collective-permute-start.7 = (f32[6,16,2,128]{3,1,2,0:T(8,128)}, f32[6,16,2,128]{3,1,2,0:T(8,128)}, u32[]{:S(2)}, u32[]{:S(2)}) collective-permute-start(f32[6,16,2,128]{3,1,2,0:T(8,128)} %copy.118), channel_id=1, source_target_pairs={{0,16},{16,32},{32,48},{1,17},{17,33},{33,49},{2,18},{18,34},{34,5... | collective-permute-start | bytes 294920 | tf_op jit(solution)/shard_map/ppermute | solution.py:17
  71.7 16.6 %collective-permute-start.10 = (f32[6,16,2,128]{3,1,2,0:T(8,128)}, f32[6,16,2,128]{3,1,2,0:T(8,128)}, u32[]{:S(2)}, u32[]{:S(2)}) collective-permute-start(f32[6,16,2,128]{3,1,2,0:T(8,128)} %copy.119), channel_id=1, source_target_pairs={{16,0},{32,16},{48,32},{17,1},{33,17},{49,33},{18,2},{34,18},{50,3... | collective-permute-start | bytes 294920 | tf_op jit(solution)/shard_map/ppermute | solution.py:18
  75.3 13.9 %collective-permute-start.8 = (f32[6,2,16,128]{3,2,1,0:T(8,128)}, f32[6,2,16,128]{3,2,1,0:T(8,128)}, u32[]{:S(2)}, u32[]{:S(2)}) collective-permute-start(f32[6,2,16,128]{3,2,1,0:T(8,128)} %get-tuple-element.54), channel_id=1, source_target_pairs={{0,64},{64,128},{128,192},{192,256},{256,320},{320,384},{384,448},... | collective-permute-start | bytes 294920 | tf_op jit(solution)/shard_map/ppermute | solution.py:17
  77.3 11.9 %collective-permute-start.9 = (f32[6,2,16,128]{3,2,1,0:T(8,128)}, f32[6,2,16,128]{3,2,1,0:T(8,128)}, u32[]{:S(2)}, u32[]{:S(2)}) collective-permute-start(f32[6,2,16,128]{3,2,1,0:T(8,128)} %get-tuple-element.55), channel_id=1, source_target_pairs={{64,0},{128,64},{192,128},{256,192},{320,256},{384,320},{448,384},... | collective-permute-start | bytes 294920 | tf_op jit(solution)/shard_map/ppermute | solution.py:18
  99.2 38.7 %collective-permute-start.12 = (f32[6,16,16,2]{2,1,3,0:T(8,128)}, f32[6,16,16,2]{2,1,3,0:T(8,128)}, u32[]{:S(2)}, u32[]{:S(2)}) collective-permute-start(f32[6,16,16,2]{2,1,3,0:T(8,128)} %copy.125), channel_id=1, source_target_pairs={{0,1},{1,2},{2,3},{3,4},{4,5},{5,6},{6,7},{7,8},{8,9},{9,10},{10,1... | collective-permute-start | bytes 36872 | tf_op jit(solution)/shard_map/ppermute | solution.py:17
  107.5 36.4 %collective-permute-start.17 = (f32[6,16,16,2]{2,1,3,0:T(8,128)}, f32[6,16,16,2]{2,1,3,0:T(8,128)}, u32[]{:S(2)}, u32[]{:S(2)}) collective-permute-start(f32[6,16,16,2]{2,1,3,0:T(8,128)} %copy.130), channel_id=1, source_target_pairs={{1,0},{2,1},{3,2},{4,3},{5,4},{6,5},{7,6},{8,7},{9,8},{10,9},{11,1... | collective-permute-start | bytes 36872 | tf_op jit(solution)/shard_map/ppermute | solution.py:18
  110.3 36.0 %collective-permute-start.13 = (f32[6,16,2,128]{3,1,2,0:T(8,128)}, f32[6,16,2,128]{3,1,2,0:T(8,128)}, u32[]{:S(2)}, u32[]{:S(2)}) collective-permute-start(f32[6,16,2,128]{3,1,2,0:T(8,128)} %copy.126), channel_id=1, source_target_pairs={{0,16},{16,32},{32,48},{1,17},{17,33},{33,49},{2,18},{18,34},{34,5... | collective-permute-start | bytes 294920 | tf_op jit(solution)/shard_map/ppermute | solution.py:17
  112.8 34.3 %collective-permute-start.16 = (f32[6,16,2,128]{3,1,2,0:T(8,128)}, f32[6,16,2,128]{3,1,2,0:T(8,128)}, u32[]{:S(2)}, u32[]{:S(2)}) collective-permute-start(f32[6,16,2,128]{3,1,2,0:T(8,128)} %copy.127), channel_id=1, source_target_pairs={{16,0},{32,16},{48,32},{17,1},{33,17},{49,33},{18,2},{34,18},{50,3... | collective-permute-start | bytes 294920 | tf_op jit(solution)/shard_map/ppermute | solution.py:18
  116.5 31.7 %collective-permute-start.14 = (f32[6,2,16,128]{3,2,1,0:T(8,128)}, f32[6,2,16,128]{3,2,1,0:T(8,128)}, u32[]{:S(2)}, u32[]{:S(2)}) collective-permute-start(f32[6,2,16,128]{3,2,1,0:T(8,128)} %get-tuple-element.48), channel_id=1, source_target_pairs={{0,64},{64,128},{128,192},{192,256},{256,320},{320,384},{384,448},... | collective-permute-start | bytes 294920 | tf_op jit(solution)/shard_map/ppermute | solution.py:17
  122.0 116.2 %all-to-all-start.1 = ((f32[15,64,4]{0,2,1:T(4,128)}), f32[15,64,4]{0,2,1:T(4,128)S(1)}, u32[]{:S(2)}, u32[]{:S(2)}) async-start(f32[15,64,4]{0,2,1:T(4,128)} %bitcast.55), calls=%async_computation.1 | async-start | bytes 262144 | tf_op jit(solution)/shard_map/all_to_all | solution.py:121
  159.6 23.2 %collective-permute-start.18 = (f32[6,16,16,2]{2,1,3,0:T(8,128)}, f32[6,16,16,2]{2,1,3,0:T(8,128)}, u32[]{:S(2)}, u32[]{:S(2)}) collective-permute-start(f32[6,16,16,2]{2,1,3,0:T(8,128)} %copy.133), channel_id=1, source_target_pairs={{0,1},{1,2},{2,3},{3,4},{4,5},{5,6},{6,7},{7,8},{8,9},{9,10},{10,1... | collective-permute-start | bytes 36872 | tf_op jit(solution)/shard_map/ppermute | solution.py:17
  166.7 22.4 %collective-permute-start.23 = (f32[6,16,16,2]{2,1,3,0:T(8,128)}, f32[6,16,16,2]{2,1,3,0:T(8,128)}, u32[]{:S(2)}, u32[]{:S(2)}) collective-permute-start(f32[6,16,16,2]{2,1,3,0:T(8,128)} %copy.138), channel_id=1, source_target_pairs={{1,0},{2,1},{3,2},{4,3},{5,4},{6,5},{7,6},{8,7},{9,8},{10,9},{11,1... | collective-permute-start | bytes 36872 | tf_op jit(solution)/shard_map/ppermute | solution.py:18
  169.5 21.9 %collective-permute-start.19 = (f32[6,16,2,128]{3,1,2,0:T(8,128)}, f32[6,16,2,128]{3,1,2,0:T(8,128)}, u32[]{:S(2)}, u32[]{:S(2)}) collective-permute-start(f32[6,16,2,128]{3,1,2,0:T(8,128)} %copy.134), channel_id=1, source_target_pairs={{0,16},{16,32},{32,48},{1,17},{17,33},{33,49},{2,18},{18,34},{34,5... | collective-permute-start | bytes 294920 | tf_op jit(solution)/shard_map/ppermute | solution.py:17
  172.1 20.3 %collective-permute-start.22 = (f32[6,16,2,128]{3,1,2,0:T(8,128)}, f32[6,16,2,128]{3,1,2,0:T(8,128)}, u32[]{:S(2)}, u32[]{:S(2)}) collective-permute-start(f32[6,16,2,128]{3,1,2,0:T(8,128)} %copy.135), channel_id=1, source_target_pairs={{16,0},{32,16},{48,32},{17,1},{33,17},{49,33},{18,2},{34,18},{50,3... | collective-permute-start | bytes 294920 | tf_op jit(solution)/shard_map/ppermute | solution.py:18
  175.7 17.6 %collective-permute-start.20 = (f32[6,2,16,128]{3,2,1,0:T(8,128)}, f32[6,2,16,128]{3,2,1,0:T(8,128)}, u32[]{:S(2)}, u32[]{:S(2)}) collective-permute-start(f32[6,2,16,128]{3,2,1,0:T(8,128)} %get-tuple-element.42), channel_id=1, source_target_pairs={{0,64},{64,128},{128,192},{192,256},{256,320},{320,384},{384,448},... | collective-permute-start | bytes 294920 | tf_op jit(solution)/shard_map/ppermute | solution.py:17
  345.9 30.3 %all-to-all-start.2 = ((f32[6,64,4]{0,2,1:T(4,128)}), f32[6,64,4]{0,2,1:T(4,128)S(1)}, u32[]{:S(2)}, u32[]{:S(2)}) async-start(f32[6,64,4]{0,2,1:T(4,128)} %bitcast.59), calls=%async_computation.2 | async-start | bytes 262144 | tf_op jit(solution)/shard_map/all_to_all | solution.py:127
  (19 other events, 225.5 us)
where the time goes:
time: 380 us; the launch traced here: 377 us
  local copies, waits for them, and re-layouts  158 us (42%)
  starting transfers between devices  143 us (38%)
  waiting for transfers between devices  38.3 us (10%)
  other arithmetic  36.2 us (10%)
    gather x1, local copies, waits for them, and re-layouts, gather_tiles(): picked = jnp.take(flat_grid, offsets[:, None] + starts[None, :], axis=1)  67.8 us
    ppermute x12, starting transfers between devices, extended(): lax.ppermute(last, axis, up)  43.2 us
    ppermute x12, starting transfers between devices, extended(): lax.ppermute(initial, axis, [(b, a) for a, b in up])  29.6 us
    unnamed x45, local copies, waits for them, and re-layouts  29.2 us
    slice x18, local copies, waits for them, and re-layouts, extended(): last = lax.slice_in_dim(array, length - width, length, axis=dim)  21.8 us
    all_to_all x1, starting transfers between devices, local(): lax.all_to_all(corner_send, ('gy', 'gz'), split_axis=1, concat_axis=1, ti...  19.1 us
    reshape x2, local copies, waits for them, and re-layouts, gather_tiles(): flat_grid = donor_grid.reshape(components, extent_x * extent_y * extent_z)  17.3 us
    all_to_all x1, waiting for transfers between devices, local(): lax.all_to_all(values, ('gy', 'gz'), split_axis=1, concat_axis=1, tiled=T...  16.4 us
  transfers between devices with their start and end apart: 33, of which 8 were waited for; matrix products, arithmetic and copies ran while one was open for 23% of the time, Pallas kernels for 0%

commit v1 on v0

--- a/solution.py
+++ b/solution.py
@@ -115,8 +115,14 @@
         jnp.zeros((15, group_size * capacity), jnp.float32).at[:, flat_index].set(donor_weights.T)
     )
     weight_send = weight_send.reshape(15, group_size, capacity)
-    donor_corners = lax.all_to_all(
-        corner_send, ("gy", "gz"), split_axis=1, concat_axis=1, tiled=True
+    donor_corners = jnp.concatenate(
+        lax.all_to_all(
+            jnp.stack(jnp.split(corner_send, lax.axis_size(("gy", "gz")), axis=1)),
+            ("gy", "gz"),
+            0,
+            0,
+        ),
+        axis=1,
     )
     piece_weights = lax.all_to_all(
         weight_send, ("gy", "gz"), split_axis=1, concat_axis=1, tiled=True

time: 380 us -> 384 us (1.011)
  local copies, waits for them, and re-layouts: 158 us -> 163 us
    unnamed x45 -> x109, local copies, waits for them, and re-layouts: 29.2 us -> 35.1 us
  transfers between devices with their start and end apart: 33 -> 33, of which waited for: 8 -> 8; matrix products, arithmetic and copies ran while one was open for 23% -> 24% of each run, Pallas kernels for 0% -> 0%
where the time goes in v1:
time: 384 us; the launch traced here: 382 us
  local copies, waits for them, and re-layouts  163 us (42%)
  starting transfers between devices  142 us (37%)
  waiting for transfers between devices  39.5 us (10%)
  other arithmetic  35.6 us (9%)
    gather x1, local copies, waits for them, and re-layouts, gather_tiles(): picked = jnp.take(flat_grid, offsets[:, None] + starts[None, :], axis=1)  67.9 us
    ppermute x12, starting transfers between devices, extended(): lax.ppermute(last, axis, up)  41.9 us
    unnamed x109, local copies, waits for them, and re-layouts  35.1 us
    ppermute x12, starting transfers between devices, extended(): lax.ppermute(initial, axis, [(b, a) for a, b in up])  29.6 us
    slice x18, local copies, waits for them, and re-layouts, extended(): last = lax.slice_in_dim(array, length - width, length, axis=dim)  21.9 us
    all_to_all x1, starting transfers between devices, local(): lax.all_to_all(jnp.stack(jnp.split(corner_send, lax.axis_size(('gy', 'gz'...  19.1 us
    reshape x2, local copies, waits for them, and re-layouts, gather_tiles(): flat_grid = donor_grid.reshape(components, extent_x * extent_y * extent_z)  17.3 us
    all_to_all x1, waiting for transfers between devices, local(): lax.all_to_all(values, ('gy', 'gz'), split_axis=1, concat_axis=1, tiled=T...  16.4 us
  transfers between devices with their start and end apart: 33, of which 8 were waited for; matrix products, arithmetic and copies ran while one was open for 24% of the time, Pallas kernels for 0%

profile of v1, /device:TPU:14, one launch (start us, length us, event | category | flops | bytes accessed | tf_op | source)
XLA Modules:
  0.0 382.1 jit_solution(7020180445564000263)
XLA Ops:
  3.1 3.8 %collective-permute-start = (f32[6,16,16,2]{2,1,3,0:T(8,128)S(1)}, f32[6,16,16,2]{2,1,3,0:T(8,128)S(1)}, u32[]{:S(2)}, u32[]{:S(2)}) collective-permute-start(f32[6,16,16,2]{2,1,3,0:T(8,128)S(1)} %copy.721), channel_id=1, source_target_pairs={{0,1},{1,2},{2,3},{3,4},{4,5},{5,6},{6,7},{7,8},{8,9},{9,10},{10,1... | collective-permute-start | bytes 36872 | tf_op jit(solution)/shard_map/ppermute | solution.py:17
  10.9 3.6 collective-permute-start.4
  14.6 4.1 %collective-permute-start.2 = (f32[6,2,16,128]{3,2,1,0:T(8,128)S(1)}, f32[6,2,16,128]{3,2,1,0:T(8,128)S(1)}, u32[]{:S(2)}, u32[]{:S(2)}) collective-permute-start(f32[6,2,16,128]{3,2,1,0:T(8,128)S(1)} %get-tuple-element.62), channel_id=1, source_target_pairs={{0,64},{64,128},{128,192},{192,256},{256,320},{320,384},{384,448},... | collective-permute-start | bytes 294920 | tf_op jit(solution)/shard_map/ppermute | solution.py:17
  27.2 19.1 %all-to-all-start = ((s32[64,3,1,4]{3,2,1,0:T(1,128)}), s32[64,3,1,4]{3,2,1,0:T(1,128)S(1)}, u32[]{:S(2)}, u32[]{:S(2)}) async-start(s32[64,3,1,4]{3,2,1,0:T(1,128)} %copy.710), calls=%async_computation | async-start | bytes 196608 | tf_op jit(solution)/shard_map/all_to_all | solution.py:119
  49.8 7.2 %collective-permute-done.3 = f32[6,2,16,128]{3,2,1,0:T(8,128)S(1)} collective-permute-done((f32[6,2,16,128]{3,2,1,0:T(8,128)S(1)}, f32[6,2,16,128]{3,2,1,0:T(8,128)S(1)}, u32[]{:S(2)}, u32[]{:S(2)}) %collective-permute-start.3) | collective-permute-done | bytes 98336 | tf_op jit(solution)/shard_map/ppermute | solution.py:18
  66.3 3.9 %collective-permute-start.6 = (f32[6,16,16,2]{2,1,3,0:T(8,128)}, f32[6,16,16,2]{2,1,3,0:T(8,128)}, u32[]{:S(2)}, u32[]{:S(2)}) collective-permute-start(f32[6,16,16,2]{2,1,3,0:T(8,128)} %copy.621), channel_id=1, source_target_pairs={{0,1},{1,2},{2,3},{3,4},{4,5},{5,6},{6,7},{7,8},{8,9},{9,10},{10,1... | collective-permute-start | bytes 36872 | tf_op jit(solution)/shard_map/ppermute | solution.py:17
  77.6 3.6 collective-permute-start.10
  83.1 3.9 %collective-permute-start.9 = (f32[6,2,16,128]{3,2,1,0:T(8,128)}, f32[6,2,16,128]{3,2,1,0:T(8,128)}, u32[]{:S(2)}, u32[]{:S(2)}) collective-permute-start(f32[6,2,16,128]{3,2,1,0:T(8,128)} %get-tuple-element.57), channel_id=1, source_target_pairs={{64,0},{128,64},{192,128},{256,192},{320,256},{384,320},{448,384},... | collective-permute-start | bytes 294920 | tf_op jit(solution)/shard_map/ppermute | solution.py:18
  105.1 5.2 %collective-permute-start.12 = (f32[6,16,16,2]{2,1,3,0:T(8,128)}, f32[6,16,16,2]{2,1,3,0:T(8,128)}, u32[]{:S(2)}, u32[]{:S(2)}) collective-permute-start(f32[6,16,16,2]{2,1,3,0:T(8,128)} %copy.629), channel_id=1, source_target_pairs={{0,1},{1,2},{2,3},{3,4},{4,5},{5,6},{6,7},{7,8},{8,9},{9,10},{10,1... | collective-permute-start | bytes 36872 | tf_op jit(solution)/shard_map/ppermute | solution.py:17
  118.7 3.6 collective-permute-start.16
  122.3 5.5 %collective-permute-start.14 = (f32[6,2,16,128]{3,2,1,0:T(8,128)}, f32[6,2,16,128]{3,2,1,0:T(8,128)}, u32[]{:S(2)}, u32[]{:S(2)}) collective-permute-start(f32[6,2,16,128]{3,2,1,0:T(8,128)} %get-tuple-element.50), channel_id=1, source_target_pairs={{0,64},{64,128},{128,192},{192,256},{256,320},{320,384},{384,448},... | collective-permute-start | bytes 294920 | tf_op jit(solution)/shard_map/ppermute | solution.py:17
  127.9 15.9 %all-to-all-start.1 = ((f32[15,64,4]{0,2,1:T(4,128)}), f32[15,64,4]{0,2,1:T(4,128)S(1)}, u32[]{:S(2)}, u32[]{:S(2)}) async-start(f32[15,64,4]{0,2,1:T(4,128)} %bitcast.120), calls=%async_computation.1 | async-start | bytes 262144 | tf_op jit(solution)/shard_map/all_to_all | solution.py:127
  165.5 4.0 %collective-permute-start.18 = (f32[6,16,16,2]{2,1,3,0:T(8,128)}, f32[6,16,16,2]{2,1,3,0:T(8,128)}, u32[]{:S(2)}, u32[]{:S(2)}) collective-permute-start(f32[6,16,16,2]{2,1,3,0:T(8,128)} %copy.637), channel_id=1, source_target_pairs={{0,1},{1,2},{2,3},{3,4},{4,5},{5,6},{6,7},{7,8},{8,9},{9,10},{10,1... | collective-permute-start | bytes 36872 | tf_op jit(solution)/shard_map/ppermute | solution.py:17
  181.7 5.7 %collective-permute-start.20 = (f32[6,2,16,128]{3,2,1,0:T(8,128)}, f32[6,2,16,128]{3,2,1,0:T(8,128)}, u32[]{:S(2)}, u32[]{:S(2)}) collective-permute-start(f32[6,2,16,128]{3,2,1,0:T(8,128)} %get-tuple-element.44), channel_id=1, source_target_pairs={{0,64},{64,128},{128,192},{192,256},{256,320},{320,384},{384,448},... | collective-permute-start | bytes 294920 | tf_op jit(solution)/shard_map/ppermute | solution.py:17
  203.8 7.5 %collective-permute-start.24 = (f32[6,2,16,128]{3,2,1,0:T(8,128)S(1)}, f32[6,2,16,128]{3,2,1,0:T(8,128)S(1)}, u32[]{:S(2)}, u32[]{:S(2)}) collective-permute-start(f32[6,2,16,128]{3,2,1,0:T(8,128)S(1)} %get-tuple-element.42), channel_id=1, source_target_pairs={{0,64},{64,128},{128,192},{192,256},{256,320},{320,384},{384,448},... | collective-permute-start | bytes 294920 | tf_op jit(solution)/shard_map/ppermute | solution.py:37
  213.5 7.9 %collective-permute-done.25 = f32[6,2,16,128]{3,2,1,0:T(8,128)S(1)} collective-permute-done((f32[6,2,16,128]{3,2,1,0:T(8,128)S(1)}, f32[6,2,16,128]{3,2,1,0:T(8,128)S(1)}, u32[]{:S(2)}, u32[]{:S(2)}) %collective-permute-start.25) | collective-permute-done | bytes 98336 | tf_op jit(solution)/shard_map/ppermute | solution.py:39
  223.5 3.6 collective-permute-start.27
  234.4 5.2 %collective-permute-start.28 = (f32[6,20,20,2]{2,1,3,0:T(8,128)}, f32[6,20,20,2]{2,1,3,0:T(8,128)}, u32[]{:S(2)}, u32[]{:S(2)}) collective-permute-start(f32[6,20,20,2]{2,1,3,0:T(8,128)} %copy.789), channel_id=1, source_target_pairs={{0,1},{1,2},{2,3},{3,4},{4,5},{5,6},{6,7},{7,8},{8,9},{9,10},{10,1... | collective-permute-start | bytes 57608 | tf_op jit(solution)/shard_map/ppermute | solution.py:37
  251.4 4.7 %pad_maximum_fusion = f32[6,20,20,132]{3,2,1,0:T(8,128)} fusion(f32[6,20,20,2]{3,2,1,0:T(8,128)} %copy.714, f32[6,20,2,128]{3,2,1,0:T(2,128)S(1)} %collective-permute-done.27, f32[6,2,16,128]{3,2,1,0:T(8,128)S(1)} %collective-permute-done.25, f32[6,16,16,128]{3,2,1,0:T(8,128)S(1)} %multiply_add_fusion, f32[6,2,16,128]{3,2,1,0:T(8,128)S(1)} %collective-permute-done.24, ...), kind=kLoop, calls=%fused_computation.32 | loop fusion | flops 1900800 | bytes 2534400 | tf_op jit(solution)/shard_map/concatenate | solution.py:35
  259.4 14.0 %copy.715 = f32[6,52800]{0,1:T(8,128)} copy(f32[6,52800]{1,0:T(8,128)S(1)} %reshape.202) | data formatting | bytes 2534400 | tf_op jit(solution)/shard_map/reshape | solution.py:80
  273.4 67.9 %gather_fusion = f32[32000,6]{1,0:T(8,128)} fusion(f32[6,52800]{0,1:T(8,128)} %copy.715, s32[32768]{0:T(1024)S(1)} %pad_clamp_fusion), kind=kCustom, calls=%fused_computation | custom fusion | bytes 1664000 | tf_op jit(solution)/shard_map/jit(_take)/gather | solution.py:88
  341.3 7.9 %multiply_reduce_fusion = f32[6,5,5,256]{0,3,2,1:T(8,128)S(1)} fusion(f32[6,5,5,5,256]{0,4,3,2,1:T(8,128)} %bitcast.231, f32[5,256]{1,0:T(8,128)S(1)} %copy.717, pred[5,5,5,256]{3,2,1,0:T(8,128)(4,1)S(1)} %fusion.10), kind=kLoop, calls=%fused_computation.4 | loop fusion | flops 537600 | bytes 958720 | tf_op jit(solution)/shard_map/reduce_sum | solution.py:73
  350.5 13.8 %all-to-all-start.2 = ((f32[6,64,4]{0,2,1:T(4,128)}), f32[6,64,4]{0,2,1:T(4,128)S(1)}, u32[]{:S(2)}, u32[]{:S(2)}) async-start(f32[6,64,4]{0,2,1:T(4,128)} %bitcast.124), calls=%async_computation.2 | async-start | bytes 262144 | tf_op jit(solution)/shard_map/all_to_all | solution.py:133
  364.4 16.4 %all-to-all-done.2 = f32[6,64,4]{0,2,1:T(4,128)S(1)} async-done(((f32[6,64,4]{0,2,1:T(4,128)}), f32[6,64,4]{0,2,1:T(4,128)S(1)}, u32[]{:S(2)}, u32[]{:S(2)}) %all-to-all-start.2) | async-done | bytes 6176 | tf_op jit(solution)/shard_map/all_to_all | solution.py:133
  (252 shorter events, 142.1 us)
Async XLA Ops:
  3.1 43.3 %collective-permute-start = (f32[6,16,16,2]{2,1,3,0:T(8,128)S(1)}, f32[6,16,16,2]{2,1,3,0:T(8,128)S(1)}, u32[]{:S(2)}, u32[]{:S(2)}) collective-permute-start(f32[6,16,16,2]{2,1,3,0:T(8,128)S(1)} %copy.721), channel_id=1, source_target_pairs={{0,1},{1,2},{2,3},{3,4},{4,5},{5,6},{6,7},{7,8},{8,9},{9,10},{10,1... | collective-permute-start | bytes 36872 | tf_op jit(solution)/shard_map/ppermute | solution.py:17
  7.6 41.5 %collective-permute-start.5 = (f32[6,16,16,2]{2,1,3,0:T(8,128)S(1)}, f32[6,16,16,2]{2,1,3,0:T(8,128)S(1)}, u32[]{:S(2)}, u32[]{:S(2)}) collective-permute-start(f32[6,16,16,2]{2,1,3,0:T(8,128)S(1)} %copy.724), channel_id=1, source_target_pairs={{1,0},{2,1},{3,2},{4,3},{5,4},{6,5},{7,6},{8,7},{9,8},{10,9},{11,1... | collective-permute-start | bytes 36872 | tf_op jit(solution)/shard_map/ppermute | solution.py:18
  9.0 40.7 %collective-permute-start.1 = (f32[6,16,2,128]{3,1,2,0:T(8,128)S(1)}, f32[6,16,2,128]{3,1,2,0:T(8,128)S(1)}, u32[]{:S(2)}, u32[]{:S(2)}) collective-permute-start(f32[6,16,2,128]{3,1,2,0:T(8,128)S(1)} %copy.722), channel_id=1, source_target_pairs={{0,16},{16,32},{32,48},{1,17},{17,33},{33,49},{2,18},{18,34},{34,5... | collective-permute-start | bytes 294920 | tf_op jit(solution)/shard_map/ppermute | solution.py:17
  10.9 38.8 %collective-permute-start.4 = (f32[6,16,2,128]{3,1,2,0:T(8,128)S(1)}, f32[6,16,2,128]{3,1,2,0:T(8,128)S(1)}, u32[]{:S(2)}, u32[]{:S(2)}) collective-permute-start(f32[6,16,2,128]{3,1,2,0:T(8,128)S(1)} %copy.723), channel_id=1, source_target_pairs={{16,0},{32,16},{48,32},{17,1},{33,17},{49,33},{18,2},{34,18},{50,3... | collective-permute-start | bytes 294920 | tf_op jit(solution)/shard_map/ppermute | solution.py:18
  14.6 35.2 %collective-permute-start.2 = (f32[6,2,16,128]{3,2,1,0:T(8,128)S(1)}, f32[6,2,16,128]{3,2,1,0:T(8,128)S(1)}, u32[]{:S(2)}, u32[]{:S(2)}) collective-permute-start(f32[6,2,16,128]{3,2,1,0:T(8,128)S(1)} %get-tuple-element.62), channel_id=1, source_target_pairs={{0,64},{64,128},{128,192},{192,256},{256,320},{320,384},{384,448},... | collective-permute-start | bytes 294920 | tf_op jit(solution)/shard_map/ppermute | solution.py:17
  27.2 100.7 %all-to-all-start = ((s32[64,3,1,4]{3,2,1,0:T(1,128)}), s32[64,3,1,4]{3,2,1,0:T(1,128)S(1)}, u32[]{:S(2)}, u32[]{:S(2)}) async-start(s32[64,3,1,4]{3,2,1,0:T(1,128)} %copy.710), calls=%async_computation | async-start | bytes 196608 | tf_op jit(solution)/shard_map/all_to_all | solution.py:119
  66.3 16.8 %collective-permute-start.6 = (f32[6,16,16,2]{2,1,3,0:T(8,128)}, f32[6,16,16,2]{2,1,3,0:T(8,128)}, u32[]{:S(2)}, u32[]{:S(2)}) collective-permute-start(f32[6,16,16,2]{2,1,3,0:T(8,128)} %copy.621), channel_id=1, source_target_pairs={{0,1},{1,2},{2,3},{3,4},{4,5},{5,6},{6,7},{7,8},{8,9},{9,10},{10,1... | collective-permute-start | bytes 36872 | tf_op jit(solution)/shard_map/ppermute | solution.py:17
  72.2 18.6 %collective-permute-start.11 = (f32[6,16,16,2]{2,1,3,0:T(8,128)}, f32[6,16,16,2]{2,1,3,0:T(8,128)}, u32[]{:S(2)}, u32[]{:S(2)}) collective-permute-start(f32[6,16,16,2]{2,1,3,0:T(8,128)} %copy.626), channel_id=1, source_target_pairs={{1,0},{2,1},{3,2},{4,3},{5,4},{6,5},{7,6},{8,7},{9,8},{10,9},{11,1... | collective-permute-start | bytes 36872 | tf_op jit(solution)/shard_map/ppermute | solution.py:18
  75.0 18.1 %collective-permute-start.7 = (f32[6,16,2,128]{3,1,2,0:T(8,128)}, f32[6,16,2,128]{3,1,2,0:T(8,128)}, u32[]{:S(2)}, u32[]{:S(2)}) collective-permute-start(f32[6,16,2,128]{3,1,2,0:T(8,128)} %copy.622), channel_id=1, source_target_pairs={{0,16},{16,32},{32,48},{1,17},{17,33},{33,49},{2,18},{18,34},{34,5... | collective-permute-start | bytes 294920 | tf_op jit(solution)/shard_map/ppermute | solution.py:17
  77.6 16.5 %collective-permute-start.10 = (f32[6,16,2,128]{3,1,2,0:T(8,128)}, f32[6,16,2,128]{3,1,2,0:T(8,128)}, u32[]{:S(2)}, u32[]{:S(2)}) collective-permute-start(f32[6,16,2,128]{3,1,2,0:T(8,128)} %copy.623), channel_id=1, source_target_pairs={{16,0},{32,16},{48,32},{17,1},{33,17},{49,33},{18,2},{34,18},{50,3... | collective-permute-start | bytes 294920 | tf_op jit(solution)/shard_map/ppermute | solution.py:18
  81.2 13.9 %collective-permute-start.8 = (f32[6,2,16,128]{3,2,1,0:T(8,128)}, f32[6,2,16,128]{3,2,1,0:T(8,128)}, u32[]{:S(2)}, u32[]{:S(2)}) collective-permute-start(f32[6,2,16,128]{3,2,1,0:T(8,128)} %get-tuple-element.56), channel_id=1, source_target_pairs={{0,64},{64,128},{128,192},{192,256},{256,320},{320,384},{384,448},... | collective-permute-start | bytes 294920 | tf_op jit(solution)/shard_map/ppermute | solution.py:17
  83.1 11.9 %collective-permute-start.9 = (f32[6,2,16,128]{3,2,1,0:T(8,128)}, f32[6,2,16,128]{3,2,1,0:T(8,128)}, u32[]{:S(2)}, u32[]{:S(2)}) collective-permute-start(f32[6,2,16,128]{3,2,1,0:T(8,128)} %get-tuple-element.57), channel_id=1, source_target_pairs={{64,0},{128,64},{192,128},{256,192},{320,256},{384,320},{448,384},... | collective-permute-start | bytes 294920 | tf_op jit(solution)/shard_map/ppermute | solution.py:18
  105.1 38.7 %collective-permute-start.12 = (f32[6,16,16,2]{2,1,3,0:T(8,128)}, f32[6,16,16,2]{2,1,3,0:T(8,128)}, u32[]{:S(2)}, u32[]{:S(2)}) collective-permute-start(f32[6,16,16,2]{2,1,3,0:T(8,128)} %copy.629), channel_id=1, source_target_pairs={{0,1},{1,2},{2,3},{3,4},{4,5},{5,6},{6,7},{7,8},{8,9},{9,10},{10,1... | collective-permute-start | bytes 36872 | tf_op jit(solution)/shard_map/ppermute | solution.py:17
  113.3 35.1 %collective-permute-start.17 = (f32[6,16,16,2]{2,1,3,0:T(8,128)}, f32[6,16,16,2]{2,1,3,0:T(8,128)}, u32[]{:S(2)}, u32[]{:S(2)}) collective-permute-start(f32[6,16,16,2]{2,1,3,0:T(8,128)} %copy.634), channel_id=1, source_target_pairs={{1,0},{2,1},{3,2},{4,3},{5,4},{6,5},{7,6},{8,7},{9,8},{10,9},{11,1... | collective-permute-start | bytes 36872 | tf_op jit(solution)/shard_map/ppermute | solution.py:18
  116.2 34.6 %collective-permute-start.13 = (f32[6,16,2,128]{3,1,2,0:T(8,128)}, f32[6,16,2,128]{3,1,2,0:T(8,128)}, u32[]{:S(2)}, u32[]{:S(2)}) collective-permute-start(f32[6,16,2,128]{3,1,2,0:T(8,128)} %copy.630), channel_id=1, source_target_pairs={{0,16},{16,32},{32,48},{1,17},{17,33},{33,49},{2,18},{18,34},{34,5... | collective-permute-start | bytes 294920 | tf_op jit(solution)/shard_map/ppermute | solution.py:17
  118.7 33.0 %collective-permute-start.16 = (f32[6,16,2,128]{3,1,2,0:T(8,128)}, f32[6,16,2,128]{3,1,2,0:T(8,128)}, u32[]{:S(2)}, u32[]{:S(2)}) collective-permute-start(f32[6,16,2,128]{3,1,2,0:T(8,128)} %copy.631), channel_id=1, source_target_pairs={{16,0},{32,16},{48,32},{17,1},{33,17},{49,33},{18,2},{34,18},{50,3... | collective-permute-start | bytes 294920 | tf_op jit(solution)/shard_map/ppermute | solution.py:18
  122.3 30.4 %collective-permute-start.14 = (f32[6,2,16,128]{3,2,1,0:T(8,128)}, f32[6,2,16,128]{3,2,1,0:T(8,128)}, u32[]{:S(2)}, u32[]{:S(2)}) collective-permute-start(f32[6,2,16,128]{3,2,1,0:T(8,128)} %get-tuple-element.50), channel_id=1, source_target_pairs={{0,64},{64,128},{128,192},{192,256},{256,320},{320,384},{384,448},... | collective-permute-start | bytes 294920 | tf_op jit(solution)/shard_map/ppermute | solution.py:17
  127.9 114.8 %all-to-all-start.1 = ((f32[15,64,4]{0,2,1:T(4,128)}), f32[15,64,4]{0,2,1:T(4,128)S(1)}, u32[]{:S(2)}, u32[]{:S(2)}) async-start(f32[15,64,4]{0,2,1:T(4,128)} %bitcast.120), calls=%async_computation.1 | async-start | bytes 262144 | tf_op jit(solution)/shard_map/all_to_all | solution.py:127
  165.5 21.8 %collective-permute-start.18 = (f32[6,16,16,2]{2,1,3,0:T(8,128)}, f32[6,16,16,2]{2,1,3,0:T(8,128)}, u32[]{:S(2)}, u32[]{:S(2)}) collective-permute-start(f32[6,16,16,2]{2,1,3,0:T(8,128)} %copy.637), channel_id=1, source_target_pairs={{0,1},{1,2},{2,3},{3,4},{4,5},{5,6},{6,7},{7,8},{8,9},{9,10},{10,1... | collective-permute-start | bytes 36872 | tf_op jit(solution)/shard_map/ppermute | solution.py:17
  172.6 21.0 %collective-permute-start.23 = (f32[6,16,16,2]{2,1,3,0:T(8,128)}, f32[6,16,16,2]{2,1,3,0:T(8,128)}, u32[]{:S(2)}, u32[]{:S(2)}) collective-permute-start(f32[6,16,16,2]{2,1,3,0:T(8,128)} %copy.642), channel_id=1, source_target_pairs={{1,0},{2,1},{3,2},{4,3},{5,4},{6,5},{7,6},{8,7},{9,8},{10,9},{11,1... | collective-permute-start | bytes 36872 | tf_op jit(solution)/shard_map/ppermute | solution.py:18
  175.5 20.6 %collective-permute-start.19 = (f32[6,16,2,128]{3,1,2,0:T(8,128)}, f32[6,16,2,128]{3,1,2,0:T(8,128)}, u32[]{:S(2)}, u32[]{:S(2)}) collective-permute-start(f32[6,16,2,128]{3,1,2,0:T(8,128)} %copy.638), channel_id=1, source_target_pairs={{0,16},{16,32},{32,48},{1,17},{17,33},{33,49},{2,18},{18,34},{34,5... | collective-permute-start | bytes 294920 | tf_op jit(solution)/shard_map/ppermute | solution.py:17
  178.0 19.0 %collective-permute-start.22 = (f32[6,16,2,128]{3,1,2,0:T(8,128)}, f32[6,16,2,128]{3,1,2,0:T(8,128)}, u32[]{:S(2)}, u32[]{:S(2)}) collective-permute-start(f32[6,16,2,128]{3,1,2,0:T(8,128)} %copy.639), channel_id=1, source_target_pairs={{16,0},{32,16},{48,32},{17,1},{33,17},{49,33},{18,2},{34,18},{50,3... | collective-permute-start | bytes 294920 | tf_op jit(solution)/shard_map/ppermute | solution.py:18
  181.7 16.3 %collective-permute-start.20 = (f32[6,2,16,128]{3,2,1,0:T(8,128)}, f32[6,2,16,128]{3,2,1,0:T(8,128)}, u32[]{:S(2)}, u32[]{:S(2)}) collective-permute-start(f32[6,2,16,128]{3,2,1,0:T(8,128)} %get-tuple-element.44), channel_id=1, source_target_pairs={{0,64},{64,128},{128,192},{192,256},{256,320},{320,384},{384,448},... | collective-permute-start | bytes 294920 | tf_op jit(solution)/shard_map/ppermute | solution.py:17
  350.5 30.3 %all-to-all-start.2 = ((f32[6,64,4]{0,2,1:T(4,128)}), f32[6,64,4]{0,2,1:T(4,128)S(1)}, u32[]{:S(2)}, u32[]{:S(2)}) async-start(f32[6,64,4]{0,2,1:T(4,128)} %bitcast.124), calls=%async_computation.2 | async-start | bytes 262144 | tf_op jit(solution)/shard_map/all_to_all | solution.py:133
  (19 other events, 225.6 us)
